TPU v7x, 128 devices: a whole 4x4x4 slice. The times are simulated.
128 devices in a mesh: dp: 4 (over x), fsdp: 32 (over z, y, core).
Axes of the slice: x: 4, y: 4, z: 4, core: 2. Of those that a mesh axis runs over, the one named last changes fastest.
Arguments:
- gradient: bfloat16 [4, 4096, 8, 1024], P('dp', 'fsdp'), may hold values from -3 to 3
- block_owner_index: int32 [32], replicated, may hold values from 0 to 31, as said below
- block_grid_cell: int32 [32], replicated, may hold values from 0 to 31, each once
- left_eigen_basis: float32 [64, 1024, 1024], P('fsdp', None, 'dp'), may hold values from -0.1875 to 0.1875
- right_eigen_basis: float32 [64, 1024, 1024], P('fsdp', None, 'dp'), may hold values from -0.1875 to 0.1875
- left_statistic_matrix: float32 [64, 1024, 1024], P('fsdp', None, 'dp'), may hold values from -6 to 6
- right_statistic_matrix: float32 [64, 1024, 1024], P('fsdp', None, 'dp'), may hold values from -6 to 6
- first_adam_moment: float32 [64, 1024, 1024], P('fsdp', None, 'dp'), may hold values from -0.09 to 0.09
- second_adam_moment: float32 [64, 1024, 1024], P('fsdp', None, 'dp'), may hold values from 1e-05 to 0.001
Outputs:
- new_left_stat: float32 [64, 1024, 1024], P('fsdp', None, 'dp')
- new_right_stat: float32 [64, 1024, 1024], P('fsdp', None, 'dp')
- new_first: float32 [64, 1024, 1024], P('fsdp', None, 'dp')
- new_second: float32 [64, 1024, 1024], P('fsdp', None, 'dp')
- update: bfloat16 [4096, 8, 1024], P('fsdp', None, 'dp')
Inputs may be any that keep to these rules, and one draw needn't show every extreme that they name: `block_owner_index`: no fsdp index owns more than 2 blocks; a quarter of the fsdp indices own 2 blocks and a quarter own none.
All inputs are finite; a program needn't handle non-finite values.
Results may differ from a plain program's by a relative error of at most 0.013.
Values may be sent and summed in bfloat16 or wider, within the bound.
No kernel may reach another device: no remote copies, remote signals or barrier semaphores. Data moves between devices by JAX's collectives and lax.ppermute only.
A program may use at most 128 MiB of HBM per device.

v0:
```python
import jax
import jax.numpy as jnp
from jax import lax
from jax.sharding import PartitionSpec as P


def in_order(blocks, dim):
    blocks = jnp.moveaxis(blocks, 0, dim)
    dims = blocks.shape
    return blocks.reshape(*dims[:dim], dims[dim] * dims[dim + 1], *dims[dim + 2 :])


def on_gathered_pieces(array, axis, dim, work, out_dim):
    width = array.shape[dim]
    pieces = jnp.split(array, 2, axis=dim) if width % 2 == 0 else [array]
    initial = jnp.arange(lax.axis_size(axis)) * width
    blocks = [lax.all_gather(piece, axis) for piece in pieces]
    made = [jax.vmap(work)(b, initial + k * (width // len(pieces))) for k, b in enumerate(blocks)]
    return in_order(jnp.concatenate(made, axis=out_dim + 1), out_dim)


def slot_lookup_table(block_owner_index, block_grid_cell, slot_count, per_owner):
    block_ids = jnp.arange(block_owner_index.shape[0], dtype=jnp.int32)
    shared = (block_owner_index[:, None] == block_owner_index[None, :]) & (
        block_ids[None, :] < block_ids[:, None]
    )
    rank_in = jnp.sum(shared.astype(jnp.int32), axis=1)
    block_slot_index = block_owner_index * per_owner + rank_in
    slot_ids = jnp.arange(slot_count, dtype=jnp.int32)
    matches = (block_slot_index[None, :] == slot_ids[:, None]).astype(jnp.int32)
    filled_marker = jnp.sum(matches, axis=1)
    slot_grid_cell = jnp.sum(matches * block_grid_cell[None, :], axis=1)
    return (block_slot_index, filled_marker, slot_grid_cell)


def local(
    gradient,
    block_owner_index,
    block_grid_cell,
    left_eigen_basis,
    right_eigen_basis,
    left_statistic_matrix,
    right_statistic_matrix,
    first_adam_moment,
    second_adam_moment,
):
    replicas = lax.axis_size("dp")
    members = lax.axis_size("fsdp")
    member = lax.axis_index("fsdp")
    column_group = lax.axis_index("dp")
    per_owner = left_eigen_basis.shape[0]
    block = left_eigen_basis.shape[1]
    width = left_eigen_basis.shape[2]
    band_rows = gradient.shape[1]
    grid_cols = gradient.shape[2]
    bands = block // band_rows
    grid_rows = members // bands
    piece_rows = band_rows // members
    slot_count = per_owner * members
    partial_terms = gradient.reshape(band_rows, grid_cols, replicas, width).astype(jnp.float32)
    reduced = lax.psum_scatter(
        partial_terms.astype(jnp.bfloat16), "dp", scatter_dimension=2, tiled=True
    ).astype(jnp.float32)
    reduced = reduced.reshape(band_rows, grid_cols, width).astype(jnp.bfloat16)
    block_slot_index, filled_marker, slot_grid_cell = slot_lookup_table(
        block_owner_index, block_grid_cell, slot_count, per_owner
    )
    my_filled = lax.dynamic_slice_in_dim(filled_marker, member * per_owner, per_owner, 0)
    split_band = reduced.reshape(members, piece_rows, grid_cols, width)
    received = lax.all_to_all(split_band, "fsdp", split_axis=0, concat_axis=0, tiled=True)
    by_cell = received.reshape(grid_rows, bands, piece_rows, grid_cols, width)
    by_cell = jnp.transpose(by_cell, (0, 3, 1, 2, 4)).reshape(
        grid_rows * grid_cols, bands, piece_rows, width
    )
    leaving = jnp.take(by_cell, slot_grid_cell, axis=0)
    leaving = jnp.where((filled_marker > 0)[:, None, None, None], leaving, jnp.zeros_like(leaving))
    leaving = leaving.reshape(members, per_owner, bands, piece_rows, width)
    landed = lax.all_to_all(leaving, "fsdp", split_axis=0, concat_axis=0, tiled=True)
    col_piece = jnp.transpose(landed, (1, 2, 0, 3, 4)).reshape(per_owner, block, width)
    gathered = lax.all_gather(col_piece, "dp", axis=2, tiled=True)
    row_piece = lax.dynamic_slice_in_dim(gathered, column_group * width, width, 1)
    new_left = 0.95 * left_statistic_matrix + 0.05 * jnp.einsum(
        "sik,sjk->sij", gathered, row_piece, preferred_element_type=jnp.float32
    )
    new_right = 0.95 * right_statistic_matrix + 0.05 * jnp.einsum(
        "ski,skj->sij", gathered, col_piece, preferred_element_type=jnp.float32
    )
    half_turn = jnp.einsum("sik,sij->skj", left_eigen_basis, gathered.astype(jnp.float32)).astype(
        jnp.bfloat16
    )

    def turn_rows(piece, start):
        return jnp.einsum("skj,sjc->skc", piece.astype(jnp.float32), right_eigen_basis)

    turned = on_gathered_pieces(half_turn, "dp", 1, turn_rows, 1)
    new_first = 0.9 * first_adam_moment + 0.1 * turned
    new_second = 0.999 * second_adam_moment + 0.001 * turned * turned
    direction = new_first / (jnp.sqrt(new_second) + 1e-08)
    full_left = lax.all_gather(left_eigen_basis, "dp", axis=2, tiled=True)
    applied = jnp.einsum("sik,skc->sic", full_left, direction)
    piece = right_eigen_basis
    moved = lax.psum_scatter(
        jnp.einsum("sic,sjc->jsi", applied, piece), "dp", scatter_dimension=0, tiled=True
    )
    backward = jnp.transpose(moved.astype(jnp.bfloat16), (1, 2, 0))
    parted = backward.reshape(per_owner, bands, members, piece_rows, width)
    parted = jnp.transpose(parted, (2, 0, 1, 3, 4))
    parted = jnp.where((my_filled > 0)[None, :, None, None, None], parted, jnp.zeros_like(parted))
    homed = lax.all_to_all(parted, "fsdp", split_axis=0, concat_axis=0, tiled=True)
    homed = homed.reshape(slot_count, bands, piece_rows, width)
    all_cells = jnp.arange(grid_rows * grid_cols, dtype=jnp.int32)
    all_hits = (block_grid_cell[None, :] == all_cells[:, None]).astype(jnp.int32)
    cell_slot = jnp.sum(all_hits * block_slot_index[None, :], axis=1)
    per_cell = jnp.take(homed, cell_slot, axis=0).reshape(
        grid_rows, grid_cols, bands, piece_rows, width
    )
    per_cell = jnp.transpose(per_cell, (0, 2, 3, 1, 4)).reshape(
        members, piece_rows, grid_cols, width
    )
    update = lax.all_to_all(per_cell, "fsdp", split_axis=0, concat_axis=0, tiled=True).reshape(
        band_rows, grid_cols, width
    )
    return (new_left, new_right, new_first, new_second, update)


def solution(mesh):
    in_specs = (
        P("dp", "fsdp", None, None),
        P(),
        P(),
        P("fsdp", None, "dp"),
        P("fsdp", None, "dp"),
        P("fsdp", None, "dp"),
        P("fsdp", None, "dp"),
        P("fsdp", None, "dp"),
        P("fsdp", None, "dp"),
    )
    out_specs = (
        P("fsdp", None, "dp"),
        P("fsdp", None, "dp"),
        P("fsdp", None, "dp"),
        P("fsdp", None, "dp"),
        P("fsdp", None, "dp"),
    )
    return jax.shard_map(local, mesh=mesh, in_specs=in_specs, out_specs=out_specs, check_vma=False)
```

profile of v0, /device:TPU:1, one launch (start us, length us, event | category | flops | bytes accessed | tf_op | source)
XLA Modules:
  0.0 404.2 jit_solution(3661794692890048232)
XLA Ops:
  7.2 3.2 copy.61
  11.6 32.2 %reduce-scatter.3.cloned.1.call-done = bf16[128,8,1,256]{3,1,0,2:T(8,128)(2,1)} async-done(((bf16[128,8,4,256]{3,1,0,2:T(8,128)(2,1)}), bf16[128,8,1,256]{3,1,0,2:T(8,128)(2,1)}) %reduce-scatter.3.cloned.1.call-update) | async-done | bytes 524304 | tf_op jit(solution)/shard_map/reduce_scatter | solution.py:61
  43.8 7.8 %all-to-all-start = ((bf16[32,4,8,256]{3,2,1,0:T(8,128)(2,1)}), bf16[32,4,8,256]{3,2,1,0:T(8,128)(2,1)S(1)}, u32[]{:S(2)}, u32[]{:S(2)}) async-start(bf16[32,4,8,256]{3,2,1,0:T(8,128)(2,1)} %bitcast.89), calls=%async_computation.1 | async-start | bytes 1048576 | tf_op jit(solution)/shard_map/all_to_all | solution.py:70
  51.7 11.3 %all-to-all-done = bf16[32,4,8,256]{3,2,1,0:T(8,128)(2,1)S(1)} async-done(((bf16[32,4,8,256]{3,2,1,0:T(8,128)(2,1)}), bf16[32,4,8,256]{3,2,1,0:T(8,128)(2,1)S(1)}, u32[]{:S(2)}, u32[]{:S(2)}) %all-to-all-start) | async-done | bytes 524320 | tf_op jit(solution)/shard_map/all_to_all | solution.py:70
  63.3 1.6 gather_fusion
  64.9 1.4 select_select_fusion
  66.3 20.7 %all_to_all.20 = bf16[32,2,8,4,256]{4,2,3,1,0:T(8,128)(2,1)S(1)} all-to-all(bf16[32,2,8,4,256]{4,2,3,1,0:T(8,128)(2,1)S(1)} %select_select_fusion), channel_id=1, replica_groups=mesh['dp'=4,'fsdp'=32] {'fsdp'}, dimensions={0} | all-to-all | bytes 2097152 | tf_op jit(solution)/shard_map/all_to_all | solution.py:78
  87.5 1.1 reshape.101
  88.7 46.0 %all-gather.7.cloned.1.call-done = bf16[2,1024,1024]{2,1,0:T(8,128)(2,1)} async-done(((bf16[2,1024,256]{2,1,0:T(8,128)(2,1)}), bf16[2,1024,1024]{2,1,0:T(8,128)(2,1)}) %all-gather.7.cloned.1.call-update) | async-done | bytes 4194320 | tf_op jit(solution)/shard_map/all_gather | solution.py:80
  134.7 4.6 %fusion.16 = bf16[2,256,1024]{1,2,0:T(8,128)(2,1)S(1)} fusion(bf16[2,1024,1024]{2,1,0:T(8,128)(2,1)} %all-gather.7.cloned.1.call-done, f32[2,1024,256]{2,1,0:T(8,128)} %param.12), kind=kOutput, calls=%fused_computation.21 | convolution fusion | flops 1073741824 | bytes 7340032 | tf_op jit(solution)/shard_map/sik,sij->skj/dot_general | solution.py:88
  139.5 1.0 copy.68
  140.6 1.0 copy.66
  141.6 2.7 convert.4
  144.4 29.2 %all-gather.13.cloned.1.call-done = bf16[8,128,1024]{2,1,0:T(8,128)(2,1)} async-done(((bf16[2,128,1024]{2,1,0:T(8,128)(2,1)}), bf16[8,128,1024]{2,1,0:T(8,128)(2,1)}) %all-gather.13.cloned.1.call-update) | async-done | bytes 2097168 | tf_op jit(solution)/shard_map/all_gather | solution.py:17
  173.6 2.3 fusion.22
  175.9 30.6 %all-gather.11.cloned.1.call-done = bf16[8,128,1024]{2,1,0:T(8,128)(2,1)} async-done(((bf16[2,128,1024]{2,1,0:T(8,128)(2,1)}), bf16[8,128,1024]{2,1,0:T(8,128)(2,1)}) %all-gather.11.cloned.1.call-update) | async-done | bytes 2097168 | tf_op jit(solution)/shard_map/all_gather | solution.py:17
  206.5 2.3 fusion.17
  208.9 1.4 copy-done.3
  211.0 2.6 fusion
  213.6 45.1 %all-gather.9.cloned.1.call-done = bf16[2,1024,1024]{2,1,0:T(8,128)(2,1)} async-done(((bf16[2,1024,256]{2,1,0:T(8,128)(2,1)}), bf16[2,1024,1024]{2,1,0:T(8,128)(2,1)}) %all-gather.9.cloned.1.call-update) | async-done | bytes 4194320 | tf_op jit(solution)/shard_map/all_gather | solution.py:99
  258.7 9.2 %convolution_bitcast_fusion = f32[1024,2,1024]{0,2,1:T(8,128)} fusion(f32[2,1024,256]{2,1,0:T(8,128)S(1)} %copy-done, bf16[2,1024,1024]{2,1,0:T(8,128)(2,1)} %all-gather.9.cloned.1.call-done, f32[2,1024,256]{2,1,0:T(8,128)} %get-tuple-element.18, f32[2,1024,256]{2,1,0:T(8,128)} %get-tuple-element.19), kind=kOutput, calls=%fused_computation.2 | convolution fusion | flops 2148532224 | bytes 18874368 | tf_op jit(solution)/shard_map/sic,sjc->jsi/dot_general | solution.py:103
  268.2 82.6 %reduce-scatter.5.cloned.1.call-done = f32[256,2,1024]{0,2,1:T(8,128)} async-done(((f32[1024,2,1024]{0,2,1:T(8,128)}), f32[256,2,1024]{0,2,1:T(8,128)}) %reduce-scatter.5.cloned.1.call-update) | async-done | bytes 2097168 | tf_op jit(solution)/shard_map/reduce_scatter | solution.py:102
  350.9 1.7 convert_bitcast_fusion
  352.9 1.6 fusion.27
  354.5 7.8 %all-to-all-start.2 = ((bf16[32,2,8,4,256]{4,2,3,1,0:T(8,128)(2,1)}), bf16[32,2,8,4,256]{4,2,3,1,0:T(8,128)(2,1)S(1)}, u32[]{:S(2)}, u32[]{:S(2)}) async-start(bf16[32,2,8,4,256]{4,2,3,1,0:T(8,128)(2,1)} %fusion.27), calls=%async_computation.4 | async-start | bytes 2097152 | tf_op jit(solution)/shard_map/all_to_all | solution.py:109
  362.3 5.9 %multiply_add_fusion = f32[2,1024,256]{2,1,0:T(8,128)} fusion(f32[2,1024,256]{2,1,0:T(8,128)} %param.15, bf16[2,1024,1024]{2,1,0:T(8,128)(2,1)} %all-gather.7.cloned.1.call-done, bf16[2,1024,256]{2,1,0:T(8,128)(2,1)S(1)} %copy-done.2), kind=kOutput, calls=%fused_computation.18 | convolution fusion | flops 1075314688 | bytes 9437184 | tf_op jit(solution)/shard_map/ski,skj->sij/dot_general | solution.py:85
  368.2 11.1 %all-to-all-done.2 = bf16[32,2,8,4,256]{4,2,3,1,0:T(8,128)(2,1)S(1)} async-done(((bf16[32,2,8,4,256]{4,2,3,1,0:T(8,128)(2,1)}), bf16[32,2,8,4,256]{4,2,3,1,0:T(8,128)(2,1)S(1)}, u32[]{:S(2)}, u32[]{:S(2)}) %all-to-all-start.2) | async-done | bytes 1048608 | tf_op jit(solution)/shard_map/all_to_all | solution.py:109
  380.0 1.1 copy.73
  381.1 3.9 all-to-all-start.3
  385.0 6.0 %multiply_add_fusion.1 = f32[2,1024,256]{2,1,0:T(8,128)} fusion(f32[2,1024,256]{2,1,0:T(8,128)} %param.14, bf16[2,1024,1024]{2,1,0:T(8,128)(2,1)} %all-gather.7.cloned.1.call-done, s32[]{:T(128)S(6)} %select_n.66), kind=kOutput, calls=%fused_computation.19 | convolution fusion | flops 1075314688 | bytes 9437188 | tf_op jit(solution)/shard_map/sik,sjk->sij/dot_general | solution.py:82
  391.0 5.5 %all-to-all-done.3 = bf16[32,4,8,256]{3,2,1,0:T(8,128)(2,1)S(1)} async-done(((bf16[32,4,8,256]{3,2,1,0:T(8,128)(2,1)}), bf16[32,4,8,256]{3,2,1,0:T(8,128)(2,1)S(1)}, u32[]{:S(2)}, u32[]{:S(2)}) %all-to-all-start.3) | async-done | bytes 524320 | tf_op jit(solution)/shard_map/all_to_all | solution.py:120
  396.6 0.8 copy.91
  (47 shorter events, 4.5 us)
Async XLA Ops:
  7.2 166.4 %copy-start = (f32[2,1024,256]{2,1,0:T(8,128)S(1)}, f32[2,1024,256]{2,1,0:T(8,128)}, u32[]{:S(2)}) copy-start(f32[2,1024,256]{2,1,0:T(8,128)} %param.13) | copy-start | bytes 6291460
  7.2 36.6 %reduce-scatter.3.cloned.1.call-start = ((), (), s32[]{:S(2)}) async-start(), calls=%async_computation.6 | async-start | bytes 2621440 | tf_op jit(solution)/shard_map/reduce_scatter | solution.py:61
  10.4 0.7 copy-start.6
  10.4 0.8 copy-start.5
  43.8 19.2 %all-to-all-start = ((bf16[32,4,8,256]{3,2,1,0:T(8,128)(2,1)}), bf16[32,4,8,256]{3,2,1,0:T(8,128)(2,1)S(1)}, u32[]{:S(2)}, u32[]{:S(2)}) async-start(bf16[32,4,8,256]{3,2,1,0:T(8,128)(2,1)} %bitcast.89), calls=%async_computation.1 | async-start | bytes 1048576 | tf_op jit(solution)/shard_map/all_to_all | solution.py:70
  51.6 83.1 %all-gather.7.cloned.1.call-start = ((), (), s32[]{:S(2)}) async-start(), calls=%async_computation.7 | async-start | bytes 5242880 | tf_op jit(solution)/shard_map/all_gather | solution.py:80
  88.6 84.9 %all-gather.13.cloned.1.call-start = ((), (), s32[]{:S(2)}) async-start(), calls=%async_computation.11 | async-start | bytes 2621440 | tf_op jit(solution)/shard_map/all_gather | solution.py:17
  140.5 66.0 %all-gather.11.cloned.1.call-start = ((), (), s32[]{:S(2)}) async-start(), calls=%async_computation.10 | async-start | bytes 2621440 | tf_op jit(solution)/shard_map/all_gather | solution.py:17
  141.6 117.2 %all-gather.9.cloned.1.call-start = ((), (), s32[]{:S(2)}) async-start(), calls=%async_computation.8 | async-start | bytes 5242880 | tf_op jit(solution)/shard_map/all_gather | solution.py:99
  144.3 206.5 %reduce-scatter.5.cloned.1.call-start = ((), (), s32[]{:S(2)}) async-start(), calls=%async_computation.9 | async-start | bytes 10485760 | tf_op jit(solution)/shard_map/reduce_scatter | solution.py:102
  208.8 1.6 copy-start.3
  208.8 2.2 copy-start.4
  352.9 9.4 %copy-start.2 = (bf16[2,1024,256]{2,1,0:T(8,128)(2,1)S(1)}, bf16[2,1024,256]{2,1,0:T(8,128)(2,1)}, u32[]{:S(2)}) copy-start(bf16[2,1024,256]{2,1,0:T(8,128)(2,1)} %reshape.101) | copy-start | bytes 3145732
  354.5 24.8 %all-to-all-start.2 = ((bf16[32,2,8,4,256]{4,2,3,1,0:T(8,128)(2,1)}), bf16[32,2,8,4,256]{4,2,3,1,0:T(8,128)(2,1)S(1)}, u32[]{:S(2)}, u32[]{:S(2)}) async-start(bf16[32,2,8,4,256]{4,2,3,1,0:T(8,128)(2,1)} %fusion.27), calls=%async_computation.4 | async-start | bytes 2097152 | tf_op jit(solution)/shard_map/all_to_all | solution.py:109
  381.1 15.5 %all-to-all-start.3 = ((bf16[32,4,8,256]{3,2,1,0:T(8,128)(2,1)}), bf16[32,4,8,256]{3,2,1,0:T(8,128)(2,1)S(1)}, u32[]{:S(2)}, u32[]{:S(2)}) async-start(bf16[32,4,8,256]{3,2,1,0:T(8,128)(2,1)} %bitcast.28), calls=%async_computation.5 | async-start | bytes 1048576 | tf_op jit(solution)/shard_map/all_to_all | solution.py:120
  385.0 12.3 %copy-start.1 = (f32[2,1024,256]{2,1,0:T(8,128)S(1)}, f32[2,1024,256]{2,1,0:T(8,128)}, u32[]{:S(2)}) copy-start(f32[2,1024,256]{2,1,0:T(8,128)} %param.13) | copy-start | bytes 6291460
Sparse Core Ops, SparseCore 0:
  11.0 32.7 reduce-scatter.2
  88.8 45.8 all-gather.6
  140.6 32.8 all-gather.12
  175.6 30.7 all-gather.10
  208.5 50.1 all-gather.8
  268.1 82.7 reduce-scatter.4
where the time goes:
time: 405 us; the launch traced here: 404 us
  waiting for transfers between devices  294 us (73%)
  matrix products  30.3 us (7%)
  blocking collectives  20.7 us (5%)
  starting transfers between devices  19.7 us (5%)
  local copies, waits for them, and re-layouts  14.6 us (4%)
  between operations  14.3 us (4%)
  other arithmetic  10.8 us (3%)
    reduce_scatter x1, waiting for transfers between devices, local(): lax.psum_scatter(jnp.einsum('sic,sjc->jsi', applied, piece), 'dp', scatte...  82.6 us
    all_gather x2, waiting for transfers between devices, on_gathered_pieces(): blocks = [lax.all_gather(piece, axis) for piece in pieces]  59.8 us
    all_gather x1, waiting for transfers between devices, local(): gathered = lax.all_gather(col_piece, 'dp', axis=2, tiled=True)  46 us
    all_gather x1, waiting for transfers between devices, local(): full_left = lax.all_gather(left_eigen_basis, 'dp', axis=2, tiled=True)  45.1 us
    reduce_scatter x1, waiting for transfers between devices, local(): lax.psum_scatter(partial_terms.astype(jnp.bfloat16), 'dp', scatter_dimens...  32.2 us
    all_to_all x1, blocking collectives, local(): lax.all_to_all(leaving, 'fsdp', split_axis=0, concat_axis=0, tiled=True)  20.7 us
    all_to_all x1, waiting for transfers between devices, local(): lax.all_to_all(split_band, 'fsdp', split_axis=0, concat_axis=0, tiled=True)  11.3 us
    all_to_all x1, waiting for transfers between devices, local(): lax.all_to_all(parted, 'fsdp', split_axis=0, concat_axis=0, tiled=True)  11.1 us
  transfers between devices with their start and end apart: 9, of which 9 were waited for; matrix products, arithmetic and copies ran while one was open for 6% of the time, Pallas kernels for 0%

commit v1 on v0

--- a/solution.py
+++ b/solution.py
@@ -77,7 +77,7 @@
     leaving = leaving.reshape(members, per_owner, bands, piece_rows, width)
     landed = lax.all_to_all(leaving, "fsdp", split_axis=0, concat_axis=0, tiled=True)
     col_piece = jnp.transpose(landed, (1, 2, 0, 3, 4)).reshape(per_owner, block, width)
-    gathered = lax.all_gather(col_piece, "dp", axis=2, tiled=True)
+    gathered = jnp.concatenate(lax.all_gather(col_piece, "dp"), axis=2)
     row_piece = lax.dynamic_slice_in_dim(gathered, column_group * width, width, 1)
     new_left = 0.95 * left_statistic_matrix + 0.05 * jnp.einsum(
         "sik,sjk->sij", gathered, row_piece, preferred_element_type=jnp.float32

time: 405 us -> 405 us (level)
  local copies, waits for them, and re-layouts: 14.6 us -> 23.3 us
  waiting for transfers between devices: 294 us -> 287 us
  transfers between devices with their start and end apart: 9 -> 9, of which waited for: 9 -> 9; matrix products, arithmetic and copies ran while one was open for 6% -> 7% of each run, Pallas kernels for 0% -> 0%
where the time goes in v1:
time: 405 us
  waiting for transfers between devices  287 us (71%)
  matrix products  28.6 us (7%)
  local copies, waits for them, and re-layouts  23.3 us (6%)
  blocking collectives  20.7 us (5%)
  starting transfers between devices  20 us (5%)
  between operations  14.4 us (4%)
  other arithmetic  10.8 us (3%)
    reduce_scatter x1, waiting for transfers between devices, local(): lax.psum_scatter(jnp.einsum('sic,sjc->jsi', applied, piece), 'dp', scatte...  82.6 us
    all_gather x2, waiting for transfers between devices, on_gathered_pieces(): blocks = [lax.all_gather(piece, axis) for piece in pieces]  55.8 us
    all_gather x1, waiting for transfers between devices, local(): full_left = lax.all_gather(left_eigen_basis, 'dp', axis=2, tiled=True)  45 us
    all_gather x1, waiting for transfers between devices, local(): gathered = jnp.concatenate(lax.all_gather(col_piece, 'dp'), axis=2)  44 us
    reduce_scatter x1, waiting for transfers between devices, local(): lax.psum_scatter(partial_terms.astype(jnp.bfloat16), 'dp', scatter_dimens...  32.2 us
    all_to_all x1, blocking collectives, local(): lax.all_to_all(leaving, 'fsdp', split_axis=0, concat_axis=0, tiled=True)  20.7 us
    all_to_all x1, waiting for transfers between devices, local(): lax.all_to_all(split_band, 'fsdp', split_axis=0, concat_axis=0, tiled=True)  11.3 us
    all_to_all x1, waiting for transfers between devices, local(): lax.all_to_all(parted, 'fsdp', split_axis=0, concat_axis=0, tiled=True)  10.3 us
  transfers between devices with their start and end apart: 9, of which 9 were waited for; matrix products, arithmetic and copies ran while one was open for 7% of the time, Pallas kernels for 0%

profile of v1, /device:TPU:1, one launch (start us, length us, event | category | flops | bytes accessed | tf_op | source)
XLA Modules:
  0.0 404.6 jit_solution(3515564762040194707)
XLA Ops:
  7.2 3.2 copy.71
  11.6 32.2 %reduce-scatter.3.cloned.1.call-done = bf16[128,8,1,256]{3,1,0,2:T(8,128)(2,1)} async-done(((bf16[128,8,4,256]{3,1,0,2:T(8,128)(2,1)}), bf16[128,8,1,256]{3,1,0,2:T(8,128)(2,1)}) %reduce-scatter.3.cloned.1.call-update) | async-done | bytes 524304 | tf_op jit(solution)/shard_map/reduce_scatter | solution.py:61
  43.8 7.8 %all-to-all-start = ((bf16[32,4,8,256]{3,2,1,0:T(8,128)(2,1)}), bf16[32,4,8,256]{3,2,1,0:T(8,128)(2,1)S(1)}, u32[]{:S(2)}, u32[]{:S(2)}) async-start(bf16[32,4,8,256]{3,2,1,0:T(8,128)(2,1)} %bitcast.98), calls=%async_computation.1 | async-start | bytes 1048576 | tf_op jit(solution)/shard_map/all_to_all | solution.py:70
  51.7 11.3 %all-to-all-done = bf16[32,4,8,256]{3,2,1,0:T(8,128)(2,1)S(1)} async-done(((bf16[32,4,8,256]{3,2,1,0:T(8,128)(2,1)}), bf16[32,4,8,256]{3,2,1,0:T(8,128)(2,1)S(1)}, u32[]{:S(2)}, u32[]{:S(2)}) %all-to-all-start) | async-done | bytes 524320 | tf_op jit(solution)/shard_map/all_to_all | solution.py:70
  63.3 1.6 gather_fusion
  64.9 1.4 select_select_fusion
  66.3 20.7 %all_to_all.20 = bf16[32,2,8,4,256]{4,2,3,1,0:T(8,128)(2,1)S(1)} all-to-all(bf16[32,2,8,4,256]{4,2,3,1,0:T(8,128)(2,1)S(1)} %select_select_fusion), channel_id=1, replica_groups=mesh['dp'=4,'fsdp'=32] {'fsdp'}, dimensions={0} | all-to-all | bytes 2097152 | tf_op jit(solution)/shard_map/all_to_all | solution.py:78
  89.3 44.0 %all-gather.7.cloned.1.call-done = bf16[4,2,1024,256]{3,2,1,0:T(8,128)(2,1)} async-done(((bf16[1,2,1024,256]{3,2,1,0:T(8,128)(2,1)}), bf16[4,2,1024,256]{3,2,1,0:T(8,128)(2,1)}) %all-gather.7.cloned.1.call-update) | async-done | bytes 4194320 | tf_op jit(solution)/shard_map/all_gather | solution.py:80
  133.3 2.9 copy.92
  136.2 1.8 fusion.16
  138.2 1.1 fusion.39
  139.3 2.0 copy.81
  141.4 2.0 copy.79
  143.6 2.7 convert.4
  146.5 26.2 %all-gather.13.cloned.1.call-done = bf16[8,128,1024]{2,1,0:T(8,128)(2,1)} async-done(((bf16[2,128,1024]{2,1,0:T(8,128)(2,1)}), bf16[8,128,1024]{2,1,0:T(8,128)(2,1)}) %all-gather.13.cloned.1.call-update) | async-done | bytes 2097168 | tf_op jit(solution)/shard_map/all_gather | solution.py:17
  172.6 3.3 fusion.22
  175.9 29.6 %all-gather.11.cloned.1.call-done = bf16[8,128,1024]{2,1,0:T(8,128)(2,1)} async-done(((bf16[2,128,1024]{2,1,0:T(8,128)(2,1)}), bf16[8,128,1024]{2,1,0:T(8,128)(2,1)}) %all-gather.11.cloned.1.call-update) | async-done | bytes 2097168 | tf_op jit(solution)/shard_map/all_gather | solution.py:17
  205.5 2.4 fusion.17
  208.1 1.4 copy-done.5
  210.2 2.6 fusion
  212.8 45.0 %all-gather.9.cloned.1.call-done = bf16[2,1024,1024]{2,1,0:T(8,128)(2,1)} async-done(((bf16[2,1024,256]{2,1,0:T(8,128)(2,1)}), bf16[2,1024,1024]{2,1,0:T(8,128)(2,1)}) %all-gather.9.cloned.1.call-update) | async-done | bytes 4194320 | tf_op jit(solution)/shard_map/all_gather | solution.py:99
  257.8 9.2 %convolution_bitcast_fusion = f32[1024,2,1024]{0,2,1:T(8,128)} fusion(f32[2,1024,256]{2,1,0:T(8,128)S(1)} %copy-done, bf16[2,1024,1024]{2,1,0:T(8,128)(2,1)} %all-gather.9.cloned.1.call-done, f32[2,1024,256]{2,1,0:T(8,128)} %get-tuple-element.18, f32[2,1024,256]{2,1,0:T(8,128)} %get-tuple-element.19), kind=kOutput, calls=%fused_computation.2 | convolution fusion | flops 2148532224 | bytes 18874368 | tf_op jit(solution)/shard_map/sic,sjc->jsi/dot_general | solution.py:103
  267.3 82.6 %reduce-scatter.5.cloned.1.call-done = f32[256,2,1024]{0,2,1:T(8,128)} async-done(((f32[1024,2,1024]{0,2,1:T(8,128)}), f32[256,2,1024]{0,2,1:T(8,128)}) %reduce-scatter.5.cloned.1.call-update) | async-done | bytes 2097168 | tf_op jit(solution)/shard_map/reduce_scatter | solution.py:102
  350.0 1.7 convert_bitcast_fusion
  351.9 1.6 fusion.27
  353.5 7.8 %all-to-all-start.2 = ((bf16[32,2,8,4,256]{4,2,3,1,0:T(8,128)(2,1)}), bf16[32,2,8,4,256]{4,2,3,1,0:T(8,128)(2,1)}, u32[]{:S(2)}, u32[]{:S(2)}) async-start(bf16[32,2,8,4,256]{4,2,3,1,0:T(8,128)(2,1)} %fusion.27), calls=%async_computation.4 | async-start | bytes 2097152 | tf_op jit(solution)/shard_map/all_to_all | solution.py:109
  362.2 5.9 %multiply_add_fusion = f32[2,1024,256]{2,1,0:T(8,128)} fusion(f32[2,1024,256]{2,1,0:T(8,128)} %param.15, bf16[2,1024,1024]{2,1,0:T(8,128)(2,1)} %bitcast.84, bf16[2,1024,256]{2,1,0:T(8,128)(2,1)S(1)} %reshape.109), kind=kOutput, calls=%fused_computation.18 | convolution fusion | flops 1075314688 | bytes 9437184 | tf_op jit(solution)/shard_map/ski,skj->sij/dot_general | solution.py:85
  368.1 10.3 %all-to-all-done.2 = bf16[32,2,8,4,256]{4,2,3,1,0:T(8,128)(2,1)} async-done(((bf16[32,2,8,4,256]{4,2,3,1,0:T(8,128)(2,1)}), bf16[32,2,8,4,256]{4,2,3,1,0:T(8,128)(2,1)}, u32[]{:S(2)}, u32[]{:S(2)}) %all-to-all-start.2) | async-done | bytes 1048608 | tf_op jit(solution)/shard_map/all_to_all | solution.py:109
  378.4 1.8 gather_fusion.1
  381.5 3.9 all-to-all-start.3
  385.4 6.0 %multiply_add_fusion.1 = f32[2,1024,256]{2,1,0:T(8,128)} fusion(f32[2,1024,256]{2,1,0:T(8,128)} %param.14, bf16[2,1024,1024]{2,1,0:T(8,128)(2,1)} %bitcast.85, s32[]{:T(128)S(6)} %select_n.66), kind=kOutput, calls=%fused_computation.19 | convolution fusion | flops 1075314688 | bytes 9437188 | tf_op jit(solution)/shard_map/sik,sjk->sij/dot_general | solution.py:82
  391.4 5.5 %all-to-all-done.3 = bf16[32,4,8,256]{3,2,1,0:T(8,128)(2,1)S(1)} async-done(((bf16[32,4,8,256]{3,2,1,0:T(8,128)(2,1)}), bf16[32,4,8,256]{3,2,1,0:T(8,128)(2,1)S(1)}, u32[]{:S(2)}, u32[]{:S(2)}) %all-to-all-start.3) | async-done | bytes 524320 | tf_op jit(solution)/shard_map/all_to_all | solution.py:120
  (54 shorter events, 8.5 us)
Async XLA Ops:
  7.2 165.5 %copy-start = (f32[2,1024,256]{2,1,0:T(8,128)S(1)}, f32[2,1024,256]{2,1,0:T(8,128)}, u32[]{:S(2)}) copy-start(f32[2,1024,256]{2,1,0:T(8,128)} %param.13) | copy-start | bytes 6291460
  7.2 36.6 %reduce-scatter.3.cloned.1.call-start = ((), (), s32[]{:S(2)}) async-start(), calls=%async_computation.6 | async-start | bytes 2621440 | tf_op jit(solution)/shard_map/reduce_scatter | solution.py:61
  10.4 0.7 copy-start.8
  10.4 0.8 copy-start.7
  43.8 19.2 %all-to-all-start = ((bf16[32,4,8,256]{3,2,1,0:T(8,128)(2,1)}), bf16[32,4,8,256]{3,2,1,0:T(8,128)(2,1)S(1)}, u32[]{:S(2)}, u32[]{:S(2)}) async-start(bf16[32,4,8,256]{3,2,1,0:T(8,128)(2,1)} %bitcast.98), calls=%async_computation.1 | async-start | bytes 1048576 | tf_op jit(solution)/shard_map/all_to_all | solution.py:70
  51.6 81.7 %all-gather.7.cloned.1.call-start = ((), (), s32[]{:S(2)}) async-start(), calls=%async_computation.7 | async-start | bytes 5242880 | tf_op jit(solution)/shard_map/all_gather | solution.py:80
  89.2 83.4 %all-gather.13.cloned.1.call-start = ((), (), s32[]{:S(2)}) async-start(), calls=%async_computation.11 | async-start | bytes 2621440 | tf_op jit(solution)/shard_map/all_gather | solution.py:17
  133.3 2.9 copy-start.3
  136.2 2.0 copy-start.2
  141.4 64.1 %all-gather.11.cloned.1.call-start = ((), (), s32[]{:S(2)}) async-start(), calls=%async_computation.10 | async-start | bytes 2621440 | tf_op jit(solution)/shard_map/all_gather | solution.py:17
  143.5 114.3 %all-gather.9.cloned.1.call-start = ((), (), s32[]{:S(2)}) async-start(), calls=%async_computation.8 | async-start | bytes 5242880 | tf_op jit(solution)/shard_map/all_gather | solution.py:99
  146.2 203.7 %reduce-scatter.5.cloned.1.call-start = ((), (), s32[]{:S(2)}) async-start(), calls=%async_computation.9 | async-start | bytes 10485760 | tf_op jit(solution)/shard_map/reduce_scatter | solution.py:102
  205.5 2.4 copy-start.4
  207.9 1.6 copy-start.5
  207.9 2.2 copy-start.6
  353.5 24.9 %all-to-all-start.2 = ((bf16[32,2,8,4,256]{4,2,3,1,0:T(8,128)(2,1)}), bf16[32,2,8,4,256]{4,2,3,1,0:T(8,128)(2,1)}, u32[]{:S(2)}, u32[]{:S(2)}) async-start(bf16[32,2,8,4,256]{4,2,3,1,0:T(8,128)(2,1)} %fusion.27), calls=%async_computation.4 | async-start | bytes 2097152 | tf_op jit(solution)/shard_map/all_to_all | solution.py:109
  381.5 15.5 %all-to-all-start.3 = ((bf16[32,4,8,256]{3,2,1,0:T(8,128)(2,1)}), bf16[32,4,8,256]{3,2,1,0:T(8,128)(2,1)S(1)}, u32[]{:S(2)}, u32[]{:S(2)}) async-start(bf16[32,4,8,256]{3,2,1,0:T(8,128)(2,1)} %bitcast.30), calls=%async_computation.5 | async-start | bytes 1048576 | tf_op jit(solution)/shard_map/all_to_all | solution.py:120
  385.4 12.3 %copy-start.1 = (f32[2,1024,256]{2,1,0:T(8,128)S(1)}, f32[2,1024,256]{2,1,0:T(8,128)}, u32[]{:S(2)}) copy-start(f32[2,1024,256]{2,1,0:T(8,128)} %param.13) | copy-start | bytes 6291460
Sparse Core Ops, SparseCore 0:
  11.0 32.7 reduce-scatter.2
  89.3 43.8 all-gather.6
  141.5 31.0 all-gather.12
  174.7 30.7 all-gather.10
  207.6 50.1 all-gather.8
  267.2 82.7 reduce-scatter.4
